TPU v7x, 128 devices: a whole 4x4x4 slice. The times are simulated.
128 devices in a mesh: vocab: 8 (over y, z_lo), dp: 16 (over z_hi, x, core).
Axes of the slice: x: 4, y: 4, z: 4 (z_hi: 2, z_lo: 2; z = z_hi * 2 + z_lo), core: 2. Of those that a mesh axis runs over, the one named last changes fastest.
Arguments:
- grads: bfloat16 [16384, 4096], P(('vocab', 'dp')), may hold values from -6 to 6
- token_ids: int32 [16384], P(('vocab', 'dp')), may hold values from 0 to 64127, as said below
Outputs:
- grad_table: float32 [64128, 4096], P('vocab', 'dp')
- row_share: float32 [64128], P('vocab')
Inputs may be any that keep to these rules, and one draw needn't show every extreme that they name: `token_ids`: within the 128 ids of one device (aligned blocks in order) the ids never fall; at most 32 of them lie in the rows k * 8016 to (k + 1) * 8016 - 1 of any one k, and in every block some k has exactly 32.
All inputs are finite; a program needn't handle non-finite values.
Results may differ from a plain program's by a relative error of at most 0.0003.
Values may be sent and summed in bfloat16 or wider, within the bound.
A program may use at most 64 MiB of HBM per device.

v0:
```python
import math

import jax
import jax.numpy as jnp
from jax import lax
from jax.sharding import PartitionSpec as P

VOCAB_DEV = 8016
TOK_DEV = 128
CAP = 32


def bucket(id_blocks, data_blocks, n_vocab):
    owner_start = jnp.arange(n_vocab, dtype=jnp.int32) * VOCAB_DEV
    starts = jnp.sum((id_blocks[:, None, :] < owner_start[None, :, None]).astype(jnp.int32), axis=2)
    length = id_blocks.shape[1]
    finish = jnp.concatenate(
        [starts[:, 1:], jnp.full((starts.shape[0], 1), length, jnp.int32)], axis=1
    )
    amount = jnp.transpose(finish - starts, (1, 0))
    begins = jnp.transpose(starts, (1, 0))
    slot = jnp.arange(CAP, dtype=jnp.int32)
    places = begins[:, :, None] + slot[None, None, :]
    valid = slot[None, None, :] < amount[:, :, None]
    columns = jnp.arange(length, dtype=jnp.int32)
    select = (places[:, :, :, None] == columns[None, None, None, :]) & valid[:, :, :, None]
    rows = jnp.einsum(
        "vbcl,bld->vbcd",
        select.astype(data_blocks.dtype),
        data_blocks,
        preferred_element_type=jnp.float32,
    )
    rows = rows.astype(data_blocks.dtype).reshape(-1, data_blocks.shape[2])
    picked = jnp.sum(jnp.where(select, id_blocks[None, :, None, :], 0), axis=3)
    slot_ids = jnp.where(valid, picked, -1).reshape(-1)
    return (rows, slot_ids)


def local(grads, token_ids):
    n_vocab = lax.axis_size("vocab")
    n_data = lax.axis_size("dp")
    spread_ids = jnp.broadcast_to(token_ids[:, None], (token_ids.shape[0], n_data))
    split_rows, split_ids = (
        lax.all_to_all(grads, "dp", split_axis=1, concat_axis=0, tiled=True),
        lax.all_to_all(spread_ids, "dp", split_axis=1, concat_axis=0, tiled=True),
    )
    group_ids = split_ids.reshape(n_data, -1)
    group_rows = split_rows.reshape(n_data, group_ids.shape[1], split_rows.shape[1])
    rows, slot_ids = bucket(group_ids, group_rows, n_vocab)
    mine, mine_ids = (
        lax.all_to_all(rows, "vocab", split_axis=0, concat_axis=0, tiled=True),
        lax.all_to_all(slot_ids, "vocab", split_axis=0, concat_axis=0, tiled=True),
    )
    local_rows = jnp.where(mine_ids < 0, -1, mine_ids - lax.axis_index("vocab") * VOCAB_DEV)
    total = local_rows.shape[0]
    width = math.gcd(total, 512)
    row_blocks = mine.reshape(total // width, width, mine.shape[1])
    id_parts = local_rows.reshape(total // width, width)
    table_rows = jnp.arange(VOCAB_DEV, dtype=jnp.int32)

    def accumulate(carry, item):
        table, counts = carry
        block, ids = item
        onehot = ids[:, None] == table_rows[None, :]
        table = table + lax.dot_general(
            onehot.astype(block.dtype),
            block,
            (((0,), (0,)), ((), ())),
            preferred_element_type=jnp.float32,
        )
        counts = counts + jnp.sum(onehot.astype(jnp.float32), axis=0)
        return ((table, counts), None)

    start = (
        jnp.zeros((VOCAB_DEV, mine.shape[1]), jnp.float32),
        jnp.zeros((VOCAB_DEV,), jnp.float32),
    )
    (grad_table, counts), _ = lax.scan(accumulate, start, (row_blocks, id_parts))
    row_share = counts * (VOCAB_DEV / (TOK_DEV * n_data))
    return (grad_table, row_share)


def solution(mesh):
    in_specs = (P(("vocab", "dp"), None), P(("vocab", "dp")))
    out_specs = (P("vocab", "dp"), P("vocab"))
    return jax.shard_map(local, mesh=mesh, in_specs=in_specs, out_specs=out_specs, check_vma=False)
```

profile of v0, /device:TPU:1, one launch (start us, length us, event | category | flops | bytes accessed | tf_op | source)
XLA Modules:
  0.0 174.7 jit_solution(10791837729172178417)
XLA Ops:
  0.6 1.3 broadcast_in_dim.26
  1.9 9.1 %all-to-all-start = ((s32[128,16,1]{0,2,1:T(1,128)}), s32[128,16,1]{0,2,1:T(1,128)S(1)}, u32[]{:S(2)}, u32[]{:S(2)}) async-start(s32[128,16,1]{0,2,1:T(1,128)} %broadcast_in_dim.26), calls=%async_computation | async-start | bytes 16384 | tf_op jit(solution)/shard_map/all_to_all | solution.py:45
  11.1 1.6 copy.31
  12.7 1.3 copy.32
  14.0 3.9 %all-to-all-done = s32[128,16,1]{0,2,1:T(1,128)S(1)} async-done(((s32[128,16,1]{0,2,1:T(1,128)}), s32[128,16,1]{0,2,1:T(1,128)S(1)}, u32[]{:S(2)}, u32[]{:S(2)}) %all-to-all-start) | async-done | bytes 8224 | tf_op jit(solution)/shard_map/all_to_all | solution.py:45
  17.9 4.1 %all-to-all-start.2 = ((bf16[128,16,256]{2,0,1:T(8,128)(2,1)}), bf16[128,16,256]{2,0,1:T(8,128)(2,1)S(1)}, u32[]{:S(2)}, u32[]{:S(2)}) async-start(bf16[128,16,256]{2,0,1:T(8,128)(2,1)} %copy.32), calls=%async_computation.2 | async-start | bytes 2097152 | tf_op jit(solution)/shard_map/all_to_all | solution.py:44
  23.0 3.6 %select_reduce_fusion = s32[8,16,32]{2,0,1:T(8,128)S(1)} fusion(s32[16,128]{1,0:T(8,128)S(1)} %bitcast.32, s32[8,16,32]{2,0,1:T(8,128)S(1)} %iota_add_fusion, pred[8,16,32]{2,0,1:T(8,128)(4,1)S(1)} %copy.26), kind=kLoop, calls=%fused_computation.13 | loop fusion | flops 2093056 | bytes 45056 | tf_op jit(solution)/shard_map/reduce_sum | solution.py:34
  26.8 0.6 copy.28
  27.4 12.0 %all-to-all-done.2 = bf16[128,16,256]{2,0,1:T(8,128)(2,1)S(1)} async-done(((bf16[128,16,256]{2,0,1:T(8,128)(2,1)}), bf16[128,16,256]{2,0,1:T(8,128)(2,1)S(1)}, u32[]{:S(2)}, u32[]{:S(2)}) %all-to-all-start.2) | async-done | bytes 1048608 | tf_op jit(solution)/shard_map/all_to_all | solution.py:44
  39.4 4.6 %all-to-all-start.1 = ((s32[8,512,1]{1,2,0:T(1,128)}), s32[8,512,1]{1,2,0:T(1,128)S(1)}, u32[]{:S(2)}, u32[]{:S(2)}) async-start(s32[8,512,1]{1,2,0:T(1,128)} %copy.28), calls=%async_computation.1 | async-start | bytes 32768 | tf_op jit(solution)/shard_map/all_to_all | solution.py:52
  44.1 1.9 %convert_bitcast_fusion = bf16[8,16,32,256]{3,2,0,1:T(8,128)(2,1)S(1)} fusion(bf16[128,16,256]{2,0,1:T(8,128)(2,1)S(1)} %all-to-all-done.2, s32[8,16,32]{2,0,1:T(8,128)S(1)} %iota_add_fusion, pred[8,16,32]{2,0,1:T(8,128)(4,1)S(1)} %copy.26), kind=kOutput, calls=%fused_computation.12 | convolution fusion | flops 270532608 | bytes 3166208 | tf_op jit(solution)/shard_map/vbcl,bld->vbcd/dot_general | solution.py:27
  45.9 1.5 copy.33
  47.4 1.7 all-to-all-done.1
  49.1 3.6 %all-to-all-start.3 = ((bf16[8,512,256]{2,1,0:T(8,128)(2,1)}), bf16[8,512,256]{2,1,0:T(8,128)(2,1)S(1)}, u32[]{:S(2)}, u32[]{:S(2)}) async-start(bf16[8,512,256]{2,1,0:T(8,128)(2,1)} %bitcast.11), calls=%async_computation.3 | async-start | bytes 4194304 | tf_op jit(solution)/shard_map/all_to_all | solution.py:51
  52.8 29.0 %all-to-all-done.3 = bf16[8,512,256]{2,1,0:T(8,128)(2,1)S(1)} async-done(((bf16[8,512,256]{2,1,0:T(8,128)(2,1)}), bf16[8,512,256]{2,1,0:T(8,128)(2,1)S(1)}, u32[]{:S(2)}, u32[]{:S(2)}) %all-to-all-start.3) | async-done | bytes 2097184 | tf_op jit(solution)/shard_map/all_to_all | solution.py:51
  81.8 92.3 %while.13 = (s32[]{:T(128)}, f32[8016,256]{1,0:T(8,128)}, f32[8016]{0:T(1024)S(1)}, s32[8,512]{1,0:T(8,128)S(1)}, bf16[8,512,256]{2,1,0:T(8,128)(2,1)S(1)}, /*index=5*/s32[]{:T(128)}, s32[]{:T(128)}) while((s32[]{:T(128)}, f32[8016,256]{1,0:T(8,128)}, f32[8016]{0:T(1024)S(1)}, s32[8,512]{1,0:T(8,128)S(1)}, ...), condition=%wide.region_4.5_spmd.clone, body=%wide.region_2.4_spmd.clone.sunk | while | flops 2121875200 | bytes 16815464 | solution.py:78
  81.8 1.8 %fusion.23 = f32[8016]{0:T(1024)S(1)} fusion(s32[512]{0:T(512)S(1)} %bitcast.28), kind=kLoop, calls=%fused_computation.4.clone.1 | loop fusion | flops 12304560 | bytes 34112 | tf_op jit(solution)/shard_map/while/body/eval_jaxpr/reduce_sum | solution.py:71
  83.6 6.8 %fusion.22 = f32[8016,256]{1,0:T(8,128)} fusion(f32[8016,256]{1,0:T(8,128)} %get-tuple-element.106, s32[512]{0:T(512)S(1)} %bitcast.29, pred[]{:T(512)S(6)} %compare.4, bf16[8,512,256]{2,1,0:T(8,128)(2,1)S(1)} %get-tuple-element.116, s32[]{:T(128)S(6)} %copy.39), kind=kOutput, calls=%fused_computation.5.clone.1 | convolution fusion | flops 2109554688 | bytes 16680965 | tf_op jit(solution)/shard_map/while/body/eval_jaxpr/dot_general | solution.py:65
  90.4 1.8 %fusion.23 = f32[8016]{0:T(1024)S(1)} fusion(s32[512]{0:T(512)S(1)} %bitcast.28), kind=kLoop, calls=%fused_computation.4.clone.1 | loop fusion | flops 12304560 | bytes 34112 | tf_op jit(solution)/shard_map/while/body/eval_jaxpr/reduce_sum | solution.py:71
  92.2 10.1 %fusion.22 = f32[8016,256]{1,0:T(8,128)} fusion(f32[8016,256]{1,0:T(8,128)} %get-tuple-element.106, s32[512]{0:T(512)S(1)} %bitcast.29, pred[]{:T(512)S(6)} %compare.4, bf16[8,512,256]{2,1,0:T(8,128)(2,1)S(1)} %get-tuple-element.116, s32[]{:T(128)S(6)} %copy.39), kind=kOutput, calls=%fused_computation.5.clone.1 | convolution fusion | flops 2109554688 | bytes 16680965 | tf_op jit(solution)/shard_map/while/body/eval_jaxpr/dot_general | solution.py:65
  102.3 1.8 %fusion.23 = f32[8016]{0:T(1024)S(1)} fusion(s32[512]{0:T(512)S(1)} %bitcast.28), kind=kLoop, calls=%fused_computation.4.clone.1 | loop fusion | flops 12304560 | bytes 34112 | tf_op jit(solution)/shard_map/while/body/eval_jaxpr/reduce_sum | solution.py:71
  104.2 10.1 %fusion.22 = f32[8016,256]{1,0:T(8,128)} fusion(f32[8016,256]{1,0:T(8,128)} %get-tuple-element.106, s32[512]{0:T(512)S(1)} %bitcast.29, pred[]{:T(512)S(6)} %compare.4, bf16[8,512,256]{2,1,0:T(8,128)(2,1)S(1)} %get-tuple-element.116, s32[]{:T(128)S(6)} %copy.39), kind=kOutput, calls=%fused_computation.5.clone.1 | convolution fusion | flops 2109554688 | bytes 16680965 | tf_op jit(solution)/shard_map/while/body/eval_jaxpr/dot_general | solution.py:65
  114.3 1.8 %fusion.23 = f32[8016]{0:T(1024)S(1)} fusion(s32[512]{0:T(512)S(1)} %bitcast.28), kind=kLoop, calls=%fused_computation.4.clone.1 | loop fusion | flops 12304560 | bytes 34112 | tf_op jit(solution)/shard_map/while/body/eval_jaxpr/reduce_sum | solution.py:71
  116.2 10.1 %fusion.22 = f32[8016,256]{1,0:T(8,128)} fusion(f32[8016,256]{1,0:T(8,128)} %get-tuple-element.106, s32[512]{0:T(512)S(1)} %bitcast.29, pred[]{:T(512)S(6)} %compare.4, bf16[8,512,256]{2,1,0:T(8,128)(2,1)S(1)} %get-tuple-element.116, s32[]{:T(128)S(6)} %copy.39), kind=kOutput, calls=%fused_computation.5.clone.1 | convolution fusion | flops 2109554688 | bytes 16680965 | tf_op jit(solution)/shard_map/while/body/eval_jaxpr/dot_general | solution.py:65
  126.3 1.8 %fusion.23 = f32[8016]{0:T(1024)S(1)} fusion(s32[512]{0:T(512)S(1)} %bitcast.28), kind=kLoop, calls=%fused_computation.4.clone.1 | loop fusion | flops 12304560 | bytes 34112 | tf_op jit(solution)/shard_map/while/body/eval_jaxpr/reduce_sum | solution.py:71
  128.1 10.1 %fusion.22 = f32[8016,256]{1,0:T(8,128)} fusion(f32[8016,256]{1,0:T(8,128)} %get-tuple-element.106, s32[512]{0:T(512)S(1)} %bitcast.29, pred[]{:T(512)S(6)} %compare.4, bf16[8,512,256]{2,1,0:T(8,128)(2,1)S(1)} %get-tuple-element.116, s32[]{:T(128)S(6)} %copy.39), kind=kOutput, calls=%fused_computation.5.clone.1 | convolution fusion | flops 2109554688 | bytes 16680965 | tf_op jit(solution)/shard_map/while/body/eval_jaxpr/dot_general | solution.py:65
  138.2 1.8 %fusion.23 = f32[8016]{0:T(1024)S(1)} fusion(s32[512]{0:T(512)S(1)} %bitcast.28), kind=kLoop, calls=%fused_computation.4.clone.1 | loop fusion | flops 12304560 | bytes 34112 | tf_op jit(solution)/shard_map/while/body/eval_jaxpr/reduce_sum | solution.py:71
  140.1 10.1 %fusion.22 = f32[8016,256]{1,0:T(8,128)} fusion(f32[8016,256]{1,0:T(8,128)} %get-tuple-element.106, s32[512]{0:T(512)S(1)} %bitcast.29, pred[]{:T(512)S(6)} %compare.4, bf16[8,512,256]{2,1,0:T(8,128)(2,1)S(1)} %get-tuple-element.116, s32[]{:T(128)S(6)} %copy.39), kind=kOutput, calls=%fused_computation.5.clone.1 | convolution fusion | flops 2109554688 | bytes 16680965 | tf_op jit(solution)/shard_map/while/body/eval_jaxpr/dot_general | solution.py:65
  150.2 1.8 %fusion.23 = f32[8016]{0:T(1024)S(1)} fusion(s32[512]{0:T(512)S(1)} %bitcast.28), kind=kLoop, calls=%fused_computation.4.clone.1 | loop fusion | flops 12304560 | bytes 34112 | tf_op jit(solution)/shard_map/while/body/eval_jaxpr/reduce_sum | solution.py:71
  152.0 10.1 %fusion.22 = f32[8016,256]{1,0:T(8,128)} fusion(f32[8016,256]{1,0:T(8,128)} %get-tuple-element.106, s32[512]{0:T(512)S(1)} %bitcast.29, pred[]{:T(512)S(6)} %compare.4, bf16[8,512,256]{2,1,0:T(8,128)(2,1)S(1)} %get-tuple-element.116, s32[]{:T(128)S(6)} %copy.39), kind=kOutput, calls=%fused_computation.5.clone.1 | convolution fusion | flops 2109554688 | bytes 16680965 | tf_op jit(solution)/shard_map/while/body/eval_jaxpr/dot_general | solution.py:65
  162.1 1.8 %fusion.23 = f32[8016]{0:T(1024)S(1)} fusion(s32[512]{0:T(512)S(1)} %bitcast.28), kind=kLoop, calls=%fused_computation.4.clone.1 | loop fusion | flops 12304560 | bytes 34112 | tf_op jit(solution)/shard_map/while/body/eval_jaxpr/reduce_sum | solution.py:71
  164.0 10.1 %fusion.22 = f32[8016,256]{1,0:T(8,128)} fusion(f32[8016,256]{1,0:T(8,128)} %get-tuple-element.106, s32[512]{0:T(512)S(1)} %bitcast.29, pred[]{:T(512)S(6)} %compare.4, bf16[8,512,256]{2,1,0:T(8,128)(2,1)S(1)} %get-tuple-element.116, s32[]{:T(128)S(6)} %copy.39), kind=kOutput, calls=%fused_computation.5.clone.1 | convolution fusion | flops 2109554688 | bytes 16680965 | tf_op jit(solution)/shard_map/while/body/eval_jaxpr/dot_general | solution.py:65
  (35 shorter events, 1.8 us)
Async XLA Ops:
  1.9 16.1 %all-to-all-start = ((s32[128,16,1]{0,2,1:T(1,128)}), s32[128,16,1]{0,2,1:T(1,128)S(1)}, u32[]{:S(2)}, u32[]{:S(2)}) async-start(s32[128,16,1]{0,2,1:T(1,128)} %broadcast_in_dim.26), calls=%async_computation | async-start | bytes 16384 | tf_op jit(solution)/shard_map/all_to_all | solution.py:45
  17.9 21.5 %all-to-all-start.2 = ((bf16[128,16,256]{2,0,1:T(8,128)(2,1)}), bf16[128,16,256]{2,0,1:T(8,128)(2,1)S(1)}, u32[]{:S(2)}, u32[]{:S(2)}) async-start(bf16[128,16,256]{2,0,1:T(8,128)(2,1)} %copy.32), calls=%async_computation.2 | async-start | bytes 2097152 | tf_op jit(solution)/shard_map/all_to_all | solution.py:44
  39.4 9.7 %all-to-all-start.1 = ((s32[8,512,1]{1,2,0:T(1,128)}), s32[8,512,1]{1,2,0:T(1,128)S(1)}, u32[]{:S(2)}, u32[]{:S(2)}) async-start(s32[8,512,1]{1,2,0:T(1,128)} %copy.28), calls=%async_computation.1 | async-start | bytes 32768 | tf_op jit(solution)/shard_map/all_to_all | solution.py:52
  49.1 32.6 %all-to-all-start.3 = ((bf16[8,512,256]{2,1,0:T(8,128)(2,1)}), bf16[8,512,256]{2,1,0:T(8,128)(2,1)S(1)}, u32[]{:S(2)}, u32[]{:S(2)}) async-start(bf16[8,512,256]{2,1,0:T(8,128)(2,1)} %bitcast.11), calls=%async_computation.3 | async-start | bytes 4194304 | tf_op jit(solution)/shard_map/all_to_all | solution.py:51
where the time goes:
time: 176 us; the launch traced here: 175 us
  matrix products  79.3 us (45%)
  waiting for transfers between devices  46.6 us (26%)
  starting transfers between devices  21.5 us (12%)
  other arithmetic  19.7 us (11%)
  local copies, waits for them, and re-layouts  6.88 us (4%)
    dot_general x8, matrix products, accumulate(): lax.dot_general(onehot.astype(block.dtype), block, (((0,), (0,)), ((), ()...  77.5 us
    all_to_all x1, waiting for transfers between devices, local(): lax.all_to_all(rows, 'vocab', split_axis=0, concat_axis=0, tiled=True)  29 us
    reduce_sum x8, other arithmetic, accumulate(): counts = counts + jnp.sum(onehot.astype(jnp.float32), axis=0)  14.7 us
    all_to_all x1, waiting for transfers between devices, local(): lax.all_to_all(grads, 'dp', split_axis=1, concat_axis=0, tiled=True)  12 us
    all_to_all x1, starting transfers between devices, local(): lax.all_to_all(spread_ids, 'dp', split_axis=1, concat_axis=0, tiled=True)  9.12 us
    all_to_all x1, starting transfers between devices, local(): lax.all_to_all(slot_ids, 'vocab', split_axis=0, concat_axis=0, tiled=True)  4.65 us
    all_to_all x1, starting transfers between devices, local(): lax.all_to_all(grads, 'dp', split_axis=1, concat_axis=0, tiled=True)  4.11 us
    all_to_all x1, waiting for transfers between devices, local(): lax.all_to_all(spread_ids, 'dp', split_axis=1, concat_axis=0, tiled=True)  3.91 us
  transfers between devices with their start and end apart: 4, of which 4 were waited for; matrix products, arithmetic and copies ran while one was open for 7% of the time, Pallas kernels for 0%

commit v1 on v0

v1 whole, which is shorter than its diff:
```python
import functools

import jax
import jax.numpy as jnp
from jax import lax
from jax.experimental import pallas as pl
from jax.experimental.pallas import tpu as pltpu
from jax.sharding import PartitionSpec as P

VOCAB_DEV = 8016
TOK_DEV = 128
CAP = 32
COLS = 256
N_V = 8
N_D = 16
N_DEV = N_V * N_D
HI_ROWS = 64
MESH = pl.DeviceIdType.MESH
NT = (((1,), (1,)), ((), ()))

PLANE_A = [(i, 0, 0, j) for j in range(2) for i in range(4)][1:]
PLANE_B = [(0, i, j, 0) for j in range(4) for i in range(4)][1:]


def position():
    v = lax.axis_index("vocab")
    d = lax.axis_index("dp")
    return (d // 2) % 4, v // 2, 2 * (d // 8) + v % 2, d % 2


def device_at(x, y, z, c):
    return y * 2 + z % 2, ((z // 2) * 4 + x) * 2 + c


def offset(k):
    c, a, b, e = k % 2, (k // 2) % 4, (k // 8) % 4, k // 32
    return a, (a + b) % 4, (a + b + e) % 4, c


def exchange(grads_hbm, ids_ref, rows_ref, keys_ref, counts_ref, held, send, id_send, id_recv,
             load_sem, send_sem, recv_sem, id_send_sem, id_recv_sem, own_sem, far_sem):
    x, y, z, c = position()

    def there(o):
        return device_at((x + o[0]) % 4, (y + o[1]) % 4, (z + o[2]) % 4, (c + o[3]) % 2)

    barrier = pltpu.get_barrier_semaphore()
    for o in PLANE_A + PLANE_B:
        pl.semaphore_signal(barrier, inc=1, device_id=there(o), device_id_type=MESH)
    load = pltpu.make_async_copy(grads_hbm, held, load_sem)
    load.start()

    ids = ids_ref[...]
    owner = jnp.zeros_like(ids)
    for v in range(1, N_V):
        owner += (ids >= v * VOCAB_DEV).astype(jnp.int32)
    lane = lax.broadcasted_iota(jnp.int32, (1, TOK_DEV), 1)
    place = lane
    for v in range(1, N_V):
        before = jnp.sum((owner < v).astype(jnp.int32), axis=1, keepdims=True)
        place = place - jnp.where(owner == v, before, 0)
    slot = owner * CAP + place
    select = (lax.broadcasted_iota(jnp.int32, (N_V * CAP, TOK_DEV), 0) == slot).astype(jnp.bfloat16)
    inner = ids - owner * VOCAB_DEV
    mine = lax.broadcasted_iota(jnp.int32, (N_V, TOK_DEV), 0) == owner
    high = jnp.where(mine, inner // 128 + 1, 0).astype(jnp.bfloat16)
    low = jnp.where(mine, inner % 128, 0).astype(jnp.bfloat16)
    spread = (lax.broadcasted_iota(jnp.int32, (TOK_DEV, TOK_DEV), 0) % CAP == place).astype(jnp.bfloat16)
    high_at = lax.dot_general(high, spread, NT, preferred_element_type=jnp.float32)
    low_at = lax.dot_general(low, spread, NT, preferred_element_type=jnp.float32)
    slot_rows = (high_at - 1.0) * 128.0 + low_at
    slot_rows = slot_rows.astype(jnp.int32)
    for v in range(N_V):
        id_send[v] = slot_rows[v : v + 1, :]
    load.wait()
    for d in range(N_D):
        send[d] = jnp.dot(select, held[:, d * COLS : (d + 1) * COLS], preferred_element_type=jnp.float32).astype(jnp.bfloat16)

    pl.semaphore_wait(barrier, len(PLANE_A) + len(PLANE_B))
    for o in PLANE_B:
        pl.semaphore_signal(far_sem, inc=1, device_id=there(o), device_id_type=MESH)
    pl.semaphore_wait(far_sem, len(PLANE_B))

    @pl.loop(1, N_DEV)
    def _(k):
        v, d = there(offset(k))
        pltpu.make_async_remote_copy(
            id_send.at[v], id_recv.at[(k % 4) * CAP + k // 4], id_send_sem, id_recv_sem, device_id=(v, d), device_id_type=MESH
        ).start()
        pltpu.make_async_remote_copy(
            send.at[d, pl.ds(pl.multiple_of(v * CAP, CAP), CAP)], rows_ref.at[k], send_sem, recv_sem.at[k // 16],
            device_id=(v, d), device_id_type=MESH
        ).start()

    v, d = device_at(x, y, z, c)
    own = pltpu.make_async_copy(send.at[d, pl.ds(pl.multiple_of(v * CAP, CAP), CAP)], rows_ref.at[0], own_sem)
    own.start()
    id_recv[0] = id_send[v]

    id_got = id_recv.at[pl.ds(1, N_DEV - 1)]
    pltpu.make_async_copy(id_got, id_got, id_recv_sem).wait()
    group = lax.broadcasted_iota(jnp.int32, (CAP, 128), 1) // CAP
    keys = jnp.zeros((CAP, 128), jnp.int32)
    for i in range(4):
        keys = jnp.where(group == i, id_recv[i * CAP : (i + 1) * CAP, 0, :], keys)
    keys_ref[...] = keys

    tall = lax.broadcasted_iota(jnp.int32, (128, 128), 0)
    total = jnp.zeros((HI_ROWS, 128), jnp.float32)
    for q in range(CAP):
        row = keys_ref[q : q + 1, :]
        hot_high = (tall[:HI_ROWS] == row // 128).astype(jnp.bfloat16)
        hot_low = (tall == row % 128).astype(jnp.bfloat16)
        total = total + lax.dot_general(hot_high, hot_low, NT, preferred_element_type=jnp.float32)
    counts_ref[...] = total * (VOCAB_DEV / (TOK_DEV * N_D))

    own.wait()
    first = rows_ref.at[pl.ds(1, 15)]
    pltpu.make_async_copy(first, first, recv_sem.at[0]).wait()
    for g in range(1, 8):
        got = rows_ref.at[pl.ds(16 * g, 16)]
        pltpu.make_async_copy(got, got, recv_sem.at[g]).wait()
    sent = rows_ref.at[pl.ds(1, N_DEV - 1)]
    pltpu.make_async_copy(sent, sent, send_sem).wait()
    pltpu.make_async_copy(id_got, id_got, id_send_sem).wait()


TILE = 512


def scatter(rows_ref, keys_ref, table_ref):
    first = pl.program_id(0) * TILE
    at = lax.broadcasted_iota(jnp.int32, (TILE, 128), 0) + first
    total = jnp.zeros((TILE, COLS), jnp.float32)
    for g in range(8):
        hots = [(at == keys_ref[4 * g + i : 4 * g + i + 1, :]).astype(jnp.bfloat16) for i in range(4)]
        total = total + jnp.dot(
            jnp.concatenate(hots, axis=1), rows_ref[512 * g : 512 * (g + 1), :], preferred_element_type=jnp.float32
        )
    table_ref[...] = total


def local(grads, token_ids):
    vmem = pl.BlockSpec(memory_space=pltpu.VMEM)
    dma = pltpu.SemaphoreType.DMA
    rows, keys, counts = pl.pallas_call(
        exchange,
        out_shape=(
            jax.ShapeDtypeStruct((N_DEV, CAP, COLS), jnp.bfloat16),
            jax.ShapeDtypeStruct((CAP, 128), jnp.int32),
            jax.ShapeDtypeStruct((HI_ROWS, 128), jnp.float32),
        ),
        in_specs=[pl.BlockSpec(memory_space=pl.ANY), vmem],
        out_specs=(vmem, vmem, vmem),
        scratch_shapes=[
            pltpu.VMEM((TOK_DEV, N_D * COLS), jnp.bfloat16),
            pltpu.VMEM((N_D, N_V * CAP, COLS), jnp.bfloat16),
            pltpu.VMEM((N_V, 1, 128), jnp.int32),
            pltpu.VMEM((N_DEV, 1, 128), jnp.int32),
            dma, dma, dma((8,)), dma, dma, dma, pltpu.SemaphoreType.REGULAR,
        ],
        compiler_params=pltpu.CompilerParams(collective_id=0, has_side_effects=True),
        name="exchange",
    )(grads, token_ids.reshape(1, TOK_DEV))
    table = pl.pallas_call(
        scatter,
        out_shape=jax.ShapeDtypeStruct((VOCAB_DEV, COLS), jnp.float32),
        grid=(pl.cdiv(VOCAB_DEV, TILE),),
        in_specs=[
            pl.BlockSpec((N_DEV * CAP, COLS), lambda i: (0, 0)),
            pl.BlockSpec((CAP, 128), lambda i: (0, 0)),
        ],
        out_specs=pl.BlockSpec((TILE, COLS), lambda i: (i, 0)),
        name="scatter",
    )(rows.reshape(N_DEV * CAP, COLS), keys)
    return table, counts.reshape(-1)[:VOCAB_DEV]


def solution(mesh):
    in_specs = (P(("vocab", "dp"), None), P(("vocab", "dp")))
    out_specs = (P("vocab", "dp"), P("vocab"))
    return jax.shard_map(local, mesh=mesh, in_specs=in_specs, out_specs=out_specs, check_vma=False)
```

time: 176 us -> 65.5 us (0.37)
  matrix products: 79.3 us -> 0 us
  Pallas kernels: 0 us -> 64 us
  waiting for transfers between devices: 46.6 us -> 0 us
  starting transfers between devices: 21.5 us -> 0 us
  other arithmetic: 19.7 us -> 0 us
  local copies, waits for them, and re-layouts: 6.88 us -> 0.62 us
    dot_general x9 -> x0, matrix products: 79.3 us -> none  [the longest x8 77.5 us: accumulate(): lax.dot_general(onehot.astype(block.dtype), block, (((0,), (0,)), ((), ()...]
    pallas_call x0 -> x2, Pallas kernels: none -> 64 us  [the longest x1 41.4 us: local(): pl.pallas_call(exchange, out_shape=(jax.ShapeDtypeStruct((N_DEV, CAP, COL...]
    all_to_all x4 -> x0, waiting for transfers between devices: 46.6 us -> none  [the longest x1 29 us: local(): lax.all_to_all(rows, 'vocab', split_axis=0, concat_axis=0, tiled=True)]
    all_to_all x4 -> x0, starting transfers between devices: 21.5 us -> none  [the longest x1 9.12 us: local(): lax.all_to_all(spread_ids, 'dp', split_axis=1, concat_axis=0, tiled=True)]
    reduce_sum x10 -> x0, other arithmetic: 18.8 us -> none  [the longest x8 14.7 us: accumulate(): counts = counts + jnp.sum(onehot.astype(jnp.float32), axis=0)]
  transfers between devices with their start and end apart: 4 -> 0, of which waited for: 4 -> 0; matrix products, arithmetic and copies ran while one was open for 7% -> 0% of each run, Pallas kernels for 0% -> 0%
where the time goes in v1:
time: 65.5 us; the launch traced here: 65.3 us
  Pallas kernels  64 us (98%)
    pallas_call x1, Pallas kernels, local(): pl.pallas_call(exchange, out_shape=(jax.ShapeDtypeStruct((N_DEV, CAP, COL...  41.4 us
    pallas_call x1, Pallas kernels, local(): pl.pallas_call(scatter, out_shape=jax.ShapeDtypeStruct((VOCAB_DEV, COLS),...  22.6 us

profile of v1, /device:TPU:1, one launch (start us, length us, event | category | flops | bytes accessed | tf_op | source)
XLA Modules:
  0.0 65.3 jit_solution(272458834852261606)
XLA Ops:
  0.6 41.4 %exchange.1 = (bf16[128,32,256]{2,1,0:T(8,128)(2,1)}, s32[32,128]{1,0:T(8,128)}, f32[64,128]{1,0:T(8,128)}) custom-call(bf16[128,4096]{1,0:T(8,128)(2,1)} %grads_hbm.1, s32[1,128]{1,0:T(1,128)} %bitcast.6), custom_call_target="tpu_custom_call" | custom-call | tf_op jit(solution)/shard_map/exchange/pallas_call | solution.py:146
  42.0 0.0 copy-start
  42.0 22.6 %scatter.1 = f32[8016,256]{1,0:T(8,128)} custom-call(bf16[4096,256]{1,0:T(8,128)(2,1)} %bitcast.4, s32[32,128]{1,0:T(8,128)} %get-tuple-element.6.keys_ref), custom_call_target="tpu_custom_call" | custom-call | tf_op jit(solution)/shard_map/scatter/pallas_call | solution.py:165
  64.6 0.0 copy-done
  64.6 0.6 copy.5
Async XLA Ops:
  42.0 22.6 %copy-start = (f32[64,128]{1,0:T(8,128)S(1)}, f32[64,128]{1,0:T(8,128)}, u32[]{:S(2)}) copy-start(f32[64,128]{1,0:T(8,128)} %get-tuple-element.7) | copy-start | bytes 98308

commit v2 on v1

--- a/solution.py
+++ b/solution.py
@@ -15,6 +15,10 @@
 N_D = 16
 N_DEV = N_V * N_D
 HI_ROWS = 64
+PAD_ROWS = 8064
+STRIPE = 4032
+TILE = 1344
+GROUPS = 8
 MESH = pl.DeviceIdType.MESH
 NT = (((1,), (1,)), ((), ()))
 
@@ -37,7 +41,7 @@
     return a, (a + b) % 4, (a + b + e) % 4, c
 
 
-def exchange(grads_hbm, ids_ref, rows_ref, keys_ref, counts_ref, held, send, id_send, id_recv,
+def exchange(grads_hbm, ids_ref, table_ref, last_ref, keys_ref, counts_ref, held, send, id_send, id_recv, rows_ref,
              load_sem, send_sem, recv_sem, id_send_sem, id_recv_sem, own_sem, far_sem):
     x, y, z, c = position()
 
@@ -114,66 +118,81 @@
         total = total + lax.dot_general(hot_high, hot_low, NT, preferred_element_type=jnp.float32)
     counts_ref[...] = total * (VOCAB_DEV / (TOK_DEV * N_D))
 
+    def add_group(g, start):
+        rows = rows_ref[pl.ds(pl.multiple_of(16 * g, 16), 16)].reshape(16 * CAP, COLS)
+        keys = [keys_ref[pl.ds(4 * g + i, 1), :] for i in range(4)]
+
+        @pl.loop(0, PAD_ROWS // STRIPE)
+        def _(t):
+            at = lax.broadcasted_iota(jnp.int32, (STRIPE, 128), 0) + t * STRIPE
+            hot = jnp.concatenate([(at == key).astype(jnp.bfloat16) for key in keys], axis=1)
+            part = jnp.dot(hot, rows, preferred_element_type=jnp.float32)
+            here = pl.ds(pl.multiple_of(t * STRIPE, STRIPE), STRIPE)
+            if start:
+                table_ref[here, :] = part
+            else:
+                table_ref[here, :] += part
+
     own.wait()
     first = rows_ref.at[pl.ds(1, 15)]
     pltpu.make_async_copy(first, first, recv_sem.at[0]).wait()
-    for g in range(1, 8):
-        got = rows_ref.at[pl.ds(16 * g, 16)]
+    add_group(0, True)
+
+    @pl.loop(1, GROUPS - 1)
+    def _(g):
+        got = rows_ref.at[pl.ds(pl.multiple_of(16 * g, 16), 16)]
         pltpu.make_async_copy(got, got, recv_sem.at[g]).wait()
+        add_group(g, False)
+
+    got = rows_ref.at[pl.ds(16 * (GROUPS - 1), 16)]
+    pltpu.make_async_copy(got, got, recv_sem.at[GROUPS - 1]).wait()
+    last_ref[...] = rows_ref[16 * (GROUPS - 1) :].reshape(last_ref.shape)
     sent = rows_ref.at[pl.ds(1, N_DEV - 1)]
     pltpu.make_async_copy(sent, sent, send_sem).wait()
     pltpu.make_async_copy(id_got, id_got, id_send_sem).wait()
 
 
-TILE = 512
-
-
-def scatter(rows_ref, keys_ref, table_ref):
+def finish(table_ref, last_ref, keys_ref, out_ref):
     first = pl.program_id(0) * TILE
     at = lax.broadcasted_iota(jnp.int32, (TILE, 128), 0) + first
-    total = jnp.zeros((TILE, COLS), jnp.float32)
-    for g in range(8):
-        hots = [(at == keys_ref[4 * g + i : 4 * g + i + 1, :]).astype(jnp.bfloat16) for i in range(4)]
-        total = total + jnp.dot(
-            jnp.concatenate(hots, axis=1), rows_ref[512 * g : 512 * (g + 1), :], preferred_element_type=jnp.float32
-        )
-    table_ref[...] = total
+    hot = jnp.concatenate([(at == keys_ref[4 * (GROUPS - 1) + i : 4 * (GROUPS - 1) + i + 1, :]).astype(jnp.bfloat16) for i in range(4)], axis=1)
+    out_ref[...] = table_ref[pl.ds(pl.multiple_of(first, TILE), TILE), :] + jnp.dot(hot, last_ref[...], preferred_element_type=jnp.float32)
 
 
 def local(grads, token_ids):
     vmem = pl.BlockSpec(memory_space=pltpu.VMEM)
     dma = pltpu.SemaphoreType.DMA
-    rows, keys, counts = pl.pallas_call(
+    table, last, keys, counts = pl.pallas_call(
         exchange,
         out_shape=(
-            jax.ShapeDtypeStruct((N_DEV, CAP, COLS), jnp.bfloat16),
-            jax.ShapeDtypeStruct((CAP, 128), jnp.int32),
+            pltpu.VMEM((PAD_ROWS, COLS), jnp.float32),
+            pltpu.VMEM((16 * CAP, COLS), jnp.bfloat16),
+            pltpu.VMEM((CAP, 128), jnp.int32),
             jax.ShapeDtypeStruct((HI_ROWS, 128), jnp.float32),
         ),
-        in_specs=[pl.BlockSpec(memory_space=pl.ANY), vmem],
-        out_specs=(vmem, vmem, vmem),
+        in_specs=[pl.BlockSpec(memory_space=pltpu.HBM), vmem],
+        out_specs=(vmem, vmem, vmem, vmem),
         scratch_shapes=[
             pltpu.VMEM((TOK_DEV, N_D * COLS), jnp.bfloat16),
             pltpu.VMEM((N_D, N_V * CAP, COLS), jnp.bfloat16),
             pltpu.VMEM((N_V, 1, 128), jnp.int32),
             pltpu.VMEM((N_DEV, 1, 128), jnp.int32),
+            pltpu.VMEM((N_DEV, CAP, COLS), jnp.bfloat16),
             dma, dma, dma((8,)), dma, dma, dma, pltpu.SemaphoreType.REGULAR,
         ],
-        compiler_params=pltpu.CompilerParams(collective_id=0, has_side_effects=True),
+        compiler_params=pltpu.CompilerParams(collective_id=0, has_side_effects=True, vmem_limit_bytes=36 << 20),
         name="exchange",
     )(grads, token_ids.reshape(1, TOK_DEV))
-    table = pl.pallas_call(
-        scatter,
+    out = pl.pallas_call(
+        finish,
         out_shape=jax.ShapeDtypeStruct((VOCAB_DEV, COLS), jnp.float32),
-        grid=(pl.cdiv(VOCAB_DEV, TILE),),
-        in_specs=[
-            pl.BlockSpec((N_DEV * CAP, COLS), lambda i: (0, 0)),
-            pl.BlockSpec((CAP, 128), lambda i: (0, 0)),
-        ],
+        grid=(PAD_ROWS // TILE,),
+        in_specs=[vmem, vmem, vmem],
         out_specs=pl.BlockSpec((TILE, COLS), lambda i: (i, 0)),
-        name="scatter",
-    )(rows.reshape(N_DEV * CAP, COLS), keys)
-    return table, counts.reshape(-1)[:VOCAB_DEV]
+        compiler_params=pltpu.CompilerParams(vmem_limit_bytes=24 << 20),
+        name="finish",
+    )(table, last, keys)
+    return out, counts.reshape(-1)[:VOCAB_DEV]
 
 
 def solution(mesh):

time: 65.5 us -> 65.5 us (level)
  local copies, waits for them, and re-layouts: 0.62 us -> 2.49 us
  Pallas kernels: 64 us -> 62.2 us
    unnamed x3 -> x5, local copies, waits for them, and re-layouts: 0.62 us -> 2.49 us
    pallas_call x2, Pallas kernels: 64 us -> 62.2 us  [the longest x1 56.8 us: local(): pl.pallas_call(exchange, out_shape=(pltpu.VMEM((PAD_ROWS, COLS), jnp.floa...]
where the time goes in v2:
time: 65.5 us; the launch traced here: 65.3 us
  Pallas kernels  62.2 us (95%)
  local copies, waits for them, and re-layouts  2.49 us (4%)
    pallas_call x1, Pallas kernels, local(): pl.pallas_call(exchange, out_shape=(pltpu.VMEM((PAD_ROWS, COLS), jnp.floa...  56.8 us
    pallas_call x1, Pallas kernels, local(): pl.pallas_call(finish, out_shape=jax.ShapeDtypeStruct((VOCAB_DEV, COLS),...  5.34 us
    unnamed x5, local copies, waits for them, and re-layouts  2.49 us

profile of v2, /device:TPU:1, one launch (start us, length us, event | category | flops | bytes accessed | tf_op | source)
XLA Modules:
  0.0 65.3 jit_solution(13772741378829425051)
XLA Ops:
  0.6 0.0 copy-start
  0.6 1.2 %copy-done = bf16[128,4096]{1,0:T(8,128)(2,1)S(1)} copy-done((bf16[128,4096]{1,0:T(8,128)(2,1)S(1)}, bf16[128,4096]{1,0:T(8,128)(2,1)}, u32[]{:S(2)}) %copy-start) | copy-done | bytes 1048600
  1.9 0.0 copy-start.1
  1.9 0.7 %copy-done.1 = s32[128]{0:T(128)S(1)} copy-done((s32[128]{0:T(128)S(1)}, s32[128]{0:T(128)}, u32[]{:S(2)}) %copy-start.1) | copy-done | bytes 536
  2.5 56.8 %exchange.1 = (f32[8064,256]{1,0:T(8,128)S(1)}, bf16[512,256]{1,0:T(8,128)(2,1)S(1)}, s32[32,128]{1,0:T(8,128)S(1)}, f32[64,128]{1,0:T(8,128)S(1)}) custom-call(bf16[128,4096]{1,0:T(8,128)(2,1)S(1)} %copy-done, s32[1,128]{1,0:T(1,128)S(1)} %bitcast.4), custom_call_target="tpu_custom_call" | custom-call | tf_op jit(solution)/shard_map/exchange/pallas_call | solution.py:165
  59.4 5.3 %finish.1 = f32[8016,256]{1,0:T(8,128)} custom-call(f32[8064,256]{1,0:T(8,128)S(1)} %get-tuple-element.6.table_ref, bf16[512,256]{1,0:T(8,128)(2,1)S(1)} %get-tuple-element.7.last_ref, s32[32,128]{1,0:T(8,128)S(1)} %get-tuple-element.8.keys_ref), custom_call_target="tpu_custom_call" | custom-call | tf_op jit(solution)/shard_map/finish/pallas_call | solution.py:186
  64.7 0.6 copy.5
Async XLA Ops:
  0.6 1.2 %copy-start = (bf16[128,4096]{1,0:T(8,128)(2,1)S(1)}, bf16[128,4096]{1,0:T(8,128)(2,1)}, u32[]{:S(2)}) copy-start(bf16[128,4096]{1,0:T(8,128)(2,1)} %grads_hbm.1) | copy-start | bytes 3145732
  1.9 0.7 %copy-start.1 = (s32[128]{0:T(128)S(1)}, s32[128]{0:T(128)}, u32[]{:S(2)}) copy-start(s32[128]{0:T(128)} %param.3) | copy-start | bytes 1540

commit v3 on v2

v3 whole, which is shorter than its diff:
```python
import jax
import jax.numpy as jnp
from jax import lax
from jax.experimental import pallas as pl
from jax.experimental.pallas import tpu as pltpu
from jax.sharding import PartitionSpec as P

VOCAB_DEV = 8016
TOK_DEV = 128
CAP = 32
COLS = 256
N_V = 8
N_D = 16
N_DEV = N_V * N_D
HI_ROWS = 64
PAD_ROWS = 8064
STRIPE = 4032
PIECES = (1344,) * 5 + (1296,)
MESH = pl.DeviceIdType.MESH
NT = (((1,), (1,)), ((), ()))

PLANE_A = [(i, 0, 0, j) for i in range(4) for j in range(2)]
PLANE_B = [(0, i, j, 0) for i in range(4) for j in range(4)]
NEAR = PLANE_A + PLANE_B[1:]
FAR = [
    (k // 2 % 4, (k // 2 + k // 8) % 4, (k // 2 + k // 8 + k // 32) % 4, k % 2)
    for k in range(N_DEV)
]
ORDER = NEAR + [o for o in FAR if o not in NEAR]
GROUPS = [(0, 16), (16, 16), (32, 16), (48, 16), (64, 16), (80, 16), (96, 16), (112, 8), (120, 8)]
LAST = GROUPS[-1][0]


def exchange(grads_hbm, ids_hbm, table_ref, last_ref, keys_ref, share_ref, held, ids_ref, send, ids_a, ids_b, rows_ref,
             load_sem, id_load_sem, send_sem, recv_sem, a_send_sem, a_recv_sem, b_send_sem, b_recv_sem, own_sem):
    v = lax.axis_index("vocab")
    d = lax.axis_index("dp")
    y, zl, zh, x, c = v // 2, v % 2, d // 8, (d // 2) % 4, d % 2
    z = 2 * zh + zl
    at_x = [2 * lax.rem(x + i, 4) for i in range(4)]
    at_y = [2 * lax.rem(y + i, 4) for i in range(4)]
    at_z = [lax.rem(z + i, 4) for i in range(4)]
    at_c = [c, 1 - c]
    vocab_at = [[at_y[i] + lax.rem(at_z[j], 2) for j in range(4)] for i in range(4)]
    data_at = [[at_x[i] + at_c[j] for j in range(2)] for i in range(4)]
    high_at = [8 * (at_z[j] // 2) for j in range(4)]

    def there(o):
        return vocab_at[o[1]][o[2]], data_at[o[0]][o[3]] + high_at[o[2]]

    barrier = pltpu.get_barrier_semaphore()
    for o in NEAR[1:]:
        pl.semaphore_signal(barrier, inc=1, device_id=there(o), device_id_type=MESH)
    id_load = pltpu.make_async_copy(ids_hbm, ids_ref, id_load_sem)
    id_load.start()
    load = pltpu.make_async_copy(grads_hbm, held, load_sem)
    load.start()

    id_load.wait()
    ids = ids_ref[...]
    owner = jnp.zeros_like(ids)
    for i in range(1, N_V):
        owner += (ids >= i * VOCAB_DEV).astype(jnp.int32)
    place = lax.broadcasted_iota(jnp.int32, (1, TOK_DEV), 1)
    for i in range(1, N_V):
        before = jnp.sum((owner < i).astype(jnp.int32), axis=1, keepdims=True)
        place = place - jnp.where(owner == i, before, 0)
    select = (lax.broadcasted_iota(jnp.int32, (N_V * CAP, TOK_DEV), 0) == owner * CAP + place).astype(jnp.bfloat16)
    inner = ids - owner * VOCAB_DEV
    mine = lax.broadcasted_iota(jnp.int32, (N_V, TOK_DEV), 0) == owner
    high = jnp.where(mine, inner // 128 + 1, 0).astype(jnp.bfloat16)
    low = jnp.where(mine, inner % 128, 0).astype(jnp.bfloat16)
    spread = (lax.broadcasted_iota(jnp.int32, (TOK_DEV, TOK_DEV), 0) % CAP == place).astype(jnp.bfloat16)
    high_of = lax.dot_general(high, spread, NT, preferred_element_type=jnp.float32)
    low_of = lax.dot_general(low, spread, NT, preferred_element_type=jnp.float32)
    slot_rows = ((high_of - 1.0) * 128.0 + low_of).astype(jnp.int32)
    for i in range(N_V):
        ids_a[0, i] = slot_rows[i : i + 1, :]
    load.wait()
    for i in range(N_D):
        send[i] = jnp.dot(select, held[:, i * COLS : (i + 1) * COLS], preferred_element_type=jnp.float32).astype(jnp.bfloat16)

    def post(k):
        to_v, to_d = there(ORDER[k])
        group = next(g for g, (first, n) in enumerate(GROUPS) if first <= k < first + n)
        pltpu.make_async_remote_copy(
            send.at[to_d, pl.ds(pl.multiple_of(to_v * CAP, CAP), CAP)],
            last_ref.at[k - LAST] if k >= LAST else rows_ref.at[k],
            send_sem, recv_sem.at[group], device_id=(to_v, to_d), device_id_type=MESH,
        ).start()

    pl.semaphore_wait(barrier, len(NEAR) - 1)
    for i, o in enumerate(PLANE_A):
        if i:
            pltpu.make_async_remote_copy(
                ids_a.at[0], ids_a.at[i], a_send_sem, a_recv_sem, device_id=there(o), device_id_type=MESH
            ).start()
    for k in range(1, 8):
        post(k)
    own = pltpu.make_async_copy(send.at[d, pl.ds(pl.multiple_of(v * CAP, CAP), CAP)], rows_ref.at[0], own_sem)
    own.start()
    got_a = ids_a.at[pl.ds(1, 7)]
    pltpu.make_async_copy(got_a, got_a, a_recv_sem).wait()
    for i, o in enumerate(PLANE_B):
        if i:
            to_v, to_d = there(o)
            pltpu.make_async_remote_copy(
                ids_a.at[:, to_v], ids_b.at[i], b_send_sem, b_recv_sem, device_id=(to_v, to_d), device_id_type=MESH
            ).start()
    for k in range(8, len(NEAR)):
        post(k)
    ids_b[0] = ids_a[:, v]
    got_b = ids_b.at[pl.ds(1, 15)]
    pltpu.make_async_copy(got_b, got_b, b_recv_sem).wait()
    for k in range(len(NEAR), N_DEV):
        post(k)

    quarter = lax.broadcasted_iota(jnp.int32, (1, 128), 1) // CAP
    for q in range(CAP):
        key = jnp.zeros((1, 128), jnp.int32)
        for i in range(4):
            o = ORDER[4 * q + i]
            from_b = ids_b[PLANE_B.index((0, o[1], o[2], 0)), PLANE_A.index((o[0], 0, 0, o[3]))]
            key = jnp.where(quarter == i, from_b, key)
        keys_ref[q : q + 1, :] = key

    tall = lax.broadcasted_iota(jnp.int32, (128, 128), 0)
    total = jnp.zeros((HI_ROWS, 128), jnp.float32)
    for q in range(CAP):
        row = keys_ref[q : q + 1, :]
        hot_high = (tall[:HI_ROWS] == row // 128).astype(jnp.bfloat16)
        hot_low = (tall == row % 128).astype(jnp.bfloat16)
        total = total + lax.dot_general(hot_high, hot_low, NT, preferred_element_type=jnp.float32)
    share_ref[...] = total * (VOCAB_DEV / (TOK_DEV * N_D))

    def add(first, n, start=False):
        rows = rows_ref[pl.ds(first, n)].reshape(n * CAP, COLS)
        keys = [keys_ref[pl.ds(first // 4 + i, 1), :] for i in range(n // 4)]

        @pl.loop(0, PAD_ROWS // STRIPE)
        def _(t):
            at = lax.broadcasted_iota(jnp.int32, (STRIPE, 128), 0) + t * STRIPE
            hot = jnp.concatenate([(at == key).astype(jnp.bfloat16) for key in keys], axis=1)
            part = jnp.dot(hot, rows, preferred_element_type=jnp.float32)
            here = pl.ds(pl.multiple_of(t * STRIPE, STRIPE), STRIPE)
            if start:
                table_ref[here, :] = part
            else:
                table_ref[here, :] += part

    def arrived(first, n, group):
        got = rows_ref.at[pl.ds(first, n)]
        pltpu.make_async_copy(got, got, recv_sem.at[group]).wait()

    own.wait()
    arrived(1, 15, 0)
    add(0, 16, True)

    @pl.loop(1, 7)
    def _(g):
        first = pl.multiple_of(16 * g, 16)
        arrived(first, 16, g)
        add(first, 16)

    arrived(112, 8, 7)
    add(112, 8)
    pltpu.make_async_copy(last_ref, last_ref, recv_sem.at[8]).wait()
    sent = rows_ref.at[pl.ds(1, N_DEV - 1)]
    pltpu.make_async_copy(sent, sent, send_sem).wait()
    pltpu.make_async_copy(got_a, got_a, a_send_sem).wait()
    pltpu.make_async_copy(got_b, got_b, b_send_sem).wait()


def finish(table_ref, last_ref, keys_ref, share_ref, table_hbm, share_hbm, stage, sems):
    share = pltpu.make_async_copy(share_ref, share_hbm, sems.at[len(PIECES)])
    share.start()
    n = GROUPS[-1][1]
    rows = last_ref[...].reshape(n * CAP, COLS)
    first = 0
    copies = [share]
    for i, size in enumerate(PIECES):
        at = lax.broadcasted_iota(jnp.int32, (size, 128), 0) + first
        keys = [keys_ref[LAST // 4 + j : LAST // 4 + j + 1, :] for j in range(n // 4)]
        hot = jnp.concatenate([(at == key).astype(jnp.bfloat16) for key in keys], axis=1)
        here = pl.ds(first, size)
        stage[here, :] = table_ref[here, :] + jnp.dot(hot, rows, preferred_element_type=jnp.float32)
        copy = pltpu.make_async_copy(stage.at[here], table_hbm.at[here], sems.at[i])
        copy.start()
        copies.append(copy)
        first += size
    for copy in copies:
        copy.wait()


def local(grads, token_ids):
    vmem = pl.BlockSpec(memory_space=pltpu.VMEM)
    hbm = pl.BlockSpec(memory_space=pltpu.HBM)
    dma = pltpu.SemaphoreType.DMA
    table, last, keys, share = pl.pallas_call(
        exchange,
        out_shape=(
            pltpu.VMEM((PAD_ROWS, COLS), jnp.float32),
            pltpu.VMEM((GROUPS[-1][1], CAP, COLS), jnp.bfloat16),
            pltpu.VMEM((CAP, 128), jnp.int32),
            pltpu.VMEM((HI_ROWS, 128), jnp.float32),
        ),
        in_specs=[hbm, hbm],
        out_specs=(vmem, vmem, vmem, vmem),
        scratch_shapes=[
            pltpu.VMEM((TOK_DEV, N_D * COLS), jnp.bfloat16),
            pltpu.VMEM((1, TOK_DEV), jnp.int32),
            pltpu.VMEM((N_D, N_V * CAP, COLS), jnp.bfloat16),
            pltpu.VMEM((8, N_V, 1, 128), jnp.int32),
            pltpu.VMEM((16, 8, 1, 128), jnp.int32),
            pltpu.VMEM((N_DEV, CAP, COLS), jnp.bfloat16),
            dma, dma, dma, dma((len(GROUPS),)), dma, dma, dma, dma, dma,
        ],
        compiler_params=pltpu.CompilerParams(collective_id=0, has_side_effects=True, vmem_limit_bytes=36 << 20),
        name="exchange",
    )(
        pltpu.with_memory_space_constraint(grads, pltpu.HBM),
        pltpu.with_memory_space_constraint(token_ids.reshape(1, TOK_DEV), pltpu.HBM),
    )
    table, share = pl.pallas_call(
        finish,
        out_shape=(
            jax.ShapeDtypeStruct((VOCAB_DEV, COLS), jnp.float32),
            jax.ShapeDtypeStruct((HI_ROWS, 128), jnp.float32),
        ),
        in_specs=[vmem, vmem, vmem, vmem],
        out_specs=(hbm, hbm),
        scratch_shapes=[pltpu.VMEM((VOCAB_DEV, COLS), jnp.float32), dma((len(PIECES) + 1,))],
        compiler_params=pltpu.CompilerParams(vmem_limit_bytes=32 << 20),
        name="finish",
    )(table, last, keys, share)
    return table, share.reshape(-1)[:VOCAB_DEV]


def solution(mesh):
    in_specs = (P(("vocab", "dp"), None), P(("vocab", "dp")))
    out_specs = (P("vocab", "dp"), P("vocab"))
    return jax.shard_map(local, mesh=mesh, in_specs=in_specs, out_specs=out_specs, check_vma=False)
```

time: 65.5 us -> 49.5 us (0.76)
  Pallas kernels: 62.2 us -> 48.8 us
  local copies, waits for them, and re-layouts: 2.49 us -> 0 us
    pallas_call x1, Pallas kernels: 56.8 us -> 44.8 us  [local(): pl.pallas_call(exchange, out_shape=(pltpu.VMEM((PAD_ROWS, COLS), jnp.floa...]
    unnamed x5 -> x0, local copies, waits for them, and re-layouts: 2.49 us -> none
    pallas_call x1, Pallas kernels: 5.34 us -> 3.94 us  [local(): pl.pallas_call(finish, out_shape=(jax.ShapeDtypeStruct((VOCAB_DEV, COLS),...]
where the time goes in v3:
time: 49.5 us; the launch traced here: 49.4 us
  Pallas kernels  48.8 us (99%)
  between operations  0.64 us (1%)
    pallas_call x1, Pallas kernels, local(): pl.pallas_call(exchange, out_shape=(pltpu.VMEM((PAD_ROWS, COLS), jnp.floa...  44.8 us
    pallas_call x1, Pallas kernels, local(): pl.pallas_call(finish, out_shape=(jax.ShapeDtypeStruct((VOCAB_DEV, COLS),...  3.94 us

profile of v3, /device:TPU:1, one launch (start us, length us, event | category | flops | bytes accessed | tf_op | source)
XLA Modules:
  0.0 49.4 jit_solution(11231379647722637668)
XLA Ops:
  0.6 44.8 %exchange.1 = (f32[8064,256]{1,0:T(8,128)S(1)}, bf16[8,32,256]{2,1,0:T(8,128)(2,1)S(1)}, s32[32,128]{1,0:T(8,128)S(1)}, f32[64,128]{1,0:T(8,128)S(1)}) custom-call(bf16[128,4096]{1,0:T(8,128)(2,1)} %grads_hbm.1, s32[1,128]{1,0:T(1,128)} %bitcast.3), custom_call_target="tpu_custom_call" | custom-call | tf_op jit(solution)/shard_map/exchange/pallas_call | solution.py:199
  45.5 3.9 %finish.1 = (f32[8016,256]{1,0:T(8,128)}, f32[64,128]{1,0:T(8,128)}) custom-call(f32[8064,256]{1,0:T(8,128)S(1)} %get-tuple-element.8.table_ref, bf16[8,32,256]{2,1,0:T(8,128)(2,1)S(1)} %get-tuple-element.9.last_ref, s32[32,128]{1,0:T(8,128)S(1)} %get-tuple-element.10.keys_ref, f32[64,128]{1,0:T(8,128)S(1)} %get-tuple-element.11.share_ref), custom_call_target="tpu_custom_call" | custom-call | tf_op jit(solution)/shard_map/finish/pallas_call | solution.py:224

commit v4 on v3

--- a/solution.py
+++ b/solution.py
@@ -27,12 +27,13 @@
     for k in range(N_DEV)
 ]
 ORDER = NEAR + [o for o in FAR if o not in NEAR]
-GROUPS = [(0, 16), (16, 16), (32, 16), (48, 16), (64, 16), (80, 16), (96, 16), (112, 8), (120, 8)]
+GROUPS = [(0, 16), (16, 16), (32, 16), (48, 16), (64, 16), (80, 16), (96, 16), (112, 16)]
+AHEAD = 3
 LAST = GROUPS[-1][0]
 
 
-def exchange(grads_hbm, ids_hbm, table_ref, last_ref, keys_ref, share_ref, held, ids_ref, send, ids_a, ids_b, rows_ref,
-             load_sem, id_load_sem, send_sem, recv_sem, a_send_sem, a_recv_sem, b_send_sem, b_recv_sem, own_sem):
+def exchange(grads_hbm, ids_hbm, table_ref, last_ref, keys_ref, share_ref, held, ids_ref, send, id_send, id_recv, rows_ref,
+             load_sem, id_load_sem, send_sem, recv_sem, id_send_sem, id_recv_sem, own_sem, far_sem):
     v = lax.axis_index("vocab")
     d = lax.axis_index("dp")
     y, zl, zh, x, c = v // 2, v % 2, d // 8, (d // 2) % 4, d % 2
@@ -75,7 +76,7 @@
     low_of = lax.dot_general(low, spread, NT, preferred_element_type=jnp.float32)
     slot_rows = ((high_of - 1.0) * 128.0 + low_of).astype(jnp.int32)
     for i in range(N_V):
-        ids_a[0, i] = slot_rows[i : i + 1, :]
+        id_send[i] = slot_rows[i : i + 1, :]
     load.wait()
     for i in range(N_D):
         send[i] = jnp.dot(select, held[:, i * COLS : (i + 1) * COLS], preferred_element_type=jnp.float32).astype(jnp.bfloat16)
@@ -83,6 +84,9 @@
     def post(k):
         to_v, to_d = there(ORDER[k])
         group = next(g for g, (first, n) in enumerate(GROUPS) if first <= k < first + n)
+        pltpu.make_async_remote_copy(
+            id_send.at[to_v], id_recv.at[k], id_send_sem, id_recv_sem.at[group], device_id=(to_v, to_d), device_id_type=MESH
+        ).start()
         pltpu.make_async_remote_copy(
             send.at[to_d, pl.ds(pl.multiple_of(to_v * CAP, CAP), CAP)],
             last_ref.at[k - LAST] if k >= LAST else rows_ref.at[k],
@@ -90,48 +94,46 @@
         ).start()
 
     pl.semaphore_wait(barrier, len(NEAR) - 1)
-    for i, o in enumerate(PLANE_A):
-        if i:
-            pltpu.make_async_remote_copy(
-                ids_a.at[0], ids_a.at[i], a_send_sem, a_recv_sem, device_id=there(o), device_id_type=MESH
-            ).start()
-    for k in range(1, 8):
+    for o in PLANE_B[1:]:
+        pl.semaphore_signal(far_sem, inc=1, device_id=there(o), device_id_type=MESH)
+    for k in range(1, len(NEAR)):
         post(k)
     own = pltpu.make_async_copy(send.at[d, pl.ds(pl.multiple_of(v * CAP, CAP), CAP)], rows_ref.at[0], own_sem)
     own.start()
-    got_a = ids_a.at[pl.ds(1, 7)]
-    pltpu.make_async_copy(got_a, got_a, a_recv_sem).wait()
-    for i, o in enumerate(PLANE_B):
-        if i:
-            to_v, to_d = there(o)
-            pltpu.make_async_remote_copy(
-                ids_a.at[:, to_v], ids_b.at[i], b_send_sem, b_recv_sem, device_id=(to_v, to_d), device_id_type=MESH
-            ).start()
-    for k in range(8, len(NEAR)):
+    id_recv[0] = id_send[v]
+    pl.semaphore_wait(far_sem, len(PLANE_B) - 1)
+    for k in range(len(NEAR), sum(GROUPS[AHEAD - 1])):
         post(k)
-    ids_b[0] = ids_a[:, v]
-    got_b = ids_b.at[pl.ds(1, 15)]
-    pltpu.make_async_copy(got_b, got_b, b_recv_sem).wait()
-    for k in range(len(NEAR), N_DEV):
-        post(k)
+
+    def post_after(g):
+        if g + AHEAD < len(GROUPS):
+            first, n = GROUPS[g + AHEAD]
+            for k in range(first, first + n):
+                post(k)
 
     quarter = lax.broadcasted_iota(jnp.int32, (1, 128), 1) // CAP
-    for q in range(CAP):
-        key = jnp.zeros((1, 128), jnp.int32)
-        for i in range(4):
-            o = ORDER[4 * q + i]
-            from_b = ids_b[PLANE_B.index((0, o[1], o[2], 0)), PLANE_A.index((o[0], 0, 0, o[3]))]
-            key = jnp.where(quarter == i, from_b, key)
-        keys_ref[q : q + 1, :] = key
-
     tall = lax.broadcasted_iota(jnp.int32, (128, 128), 0)
-    total = jnp.zeros((HI_ROWS, 128), jnp.float32)
-    for q in range(CAP):
-        row = keys_ref[q : q + 1, :]
-        hot_high = (tall[:HI_ROWS] == row // 128).astype(jnp.bfloat16)
-        hot_low = (tall == row % 128).astype(jnp.bfloat16)
-        total = total + lax.dot_general(hot_high, hot_low, NT, preferred_element_type=jnp.float32)
-    share_ref[...] = total * (VOCAB_DEV / (TOK_DEV * N_D))
+
+    def learn(g):
+        first, n = GROUPS[g]
+        skip = int(g == 0)
+        got = id_recv.at[pl.ds(first + skip, n - skip)]
+        pltpu.make_async_copy(got, got, id_recv_sem.at[g]).wait()
+        hot_high, hot_low = [], []
+        for q in range(first // 4, (first + n) // 4):
+            key = id_recv[4 * q]
+            for i in range(1, 4):
+                key = jnp.where(quarter == i, id_recv[4 * q + i], key)
+            keys_ref[q : q + 1, :] = key
+            hot_high.append((tall[:HI_ROWS] == key // 128).astype(jnp.bfloat16))
+            hot_low.append((tall == key % 128).astype(jnp.bfloat16))
+        found = lax.dot_general(
+            jnp.concatenate(hot_high, axis=1), jnp.concatenate(hot_low, axis=1), NT, preferred_element_type=jnp.float32
+        ) * (VOCAB_DEV / (TOK_DEV * N_D))
+        if g == 0:
+            share_ref[...] = found
+        else:
+            share_ref[...] += found
 
     def add(first, n, start=False):
         rows = rows_ref[pl.ds(first, n)].reshape(n * CAP, COLS)
@@ -152,23 +154,22 @@
         got = rows_ref.at[pl.ds(first, n)]
         pltpu.make_async_copy(got, got, recv_sem.at[group]).wait()
 
+    learn(0)
     own.wait()
-    arrived(1, 15, 0)
-    add(0, 16, True)
-
-    @pl.loop(1, 7)
-    def _(g):
-        first = pl.multiple_of(16 * g, 16)
-        arrived(first, 16, g)
-        add(first, 16)
-
-    arrived(112, 8, 7)
-    add(112, 8)
-    pltpu.make_async_copy(last_ref, last_ref, recv_sem.at[8]).wait()
+    arrived(1, GROUPS[0][1] - 1, 0)
+    post_after(0)
+    add(0, GROUPS[0][1], True)
+    for g in range(1, len(GROUPS) - 1):
+        learn(g)
+        arrived(*GROUPS[g], g)
+        post_after(g)
+        add(*GROUPS[g])
+    learn(len(GROUPS) - 1)
+    pltpu.make_async_copy(last_ref, last_ref, recv_sem.at[len(GROUPS) - 1]).wait()
     sent = rows_ref.at[pl.ds(1, N_DEV - 1)]
     pltpu.make_async_copy(sent, sent, send_sem).wait()
-    pltpu.make_async_copy(got_a, got_a, a_send_sem).wait()
-    pltpu.make_async_copy(got_b, got_b, b_send_sem).wait()
+    sent_ids = id_recv.at[pl.ds(1, N_DEV - 1)]
+    pltpu.make_async_copy(sent_ids, sent_ids, id_send_sem).wait()
 
 
 def finish(table_ref, last_ref, keys_ref, share_ref, table_hbm, share_hbm, stage, sems):
@@ -210,10 +211,11 @@
             pltpu.VMEM((TOK_DEV, N_D * COLS), jnp.bfloat16),
             pltpu.VMEM((1, TOK_DEV), jnp.int32),
             pltpu.VMEM((N_D, N_V * CAP, COLS), jnp.bfloat16),
-            pltpu.VMEM((8, N_V, 1, 128), jnp.int32),
-            pltpu.VMEM((16, 8, 1, 128), jnp.int32),
+            pltpu.VMEM((N_V, 1, 128), jnp.int32),
+            pltpu.VMEM((N_DEV, 1, 128), jnp.int32),
             pltpu.VMEM((N_DEV, CAP, COLS), jnp.bfloat16),
-            dma, dma, dma, dma((len(GROUPS),)), dma, dma, dma, dma, dma,
+            dma, dma, dma, dma((len(GROUPS),)), dma, dma((len(GROUPS),)), dma,
+            pltpu.SemaphoreType.REGULAR,
         ],
         compiler_params=pltpu.CompilerParams(collective_id=0, has_side_effects=True, vmem_limit_bytes=36 << 20),
         name="exchange",

time: 49.5 us -> 46.5 us (0.939)
  Pallas kernels: 48.8 us -> 45.6 us
    pallas_call x1, Pallas kernels: 44.8 us -> 41.3 us  [local(): pl.pallas_call(exchange, out_shape=(pltpu.VMEM((PAD_ROWS, COLS), jnp.floa...]
where the time goes in v4:
time: 46.5 us; the launch traced here: 46.4 us
  Pallas kernels  45.6 us (98%)
  between operations  0.8 us (2%)
    pallas_call x1, Pallas kernels, local(): pl.pallas_call(exchange, out_shape=(pltpu.VMEM((PAD_ROWS, COLS), jnp.floa...  41.3 us
    pallas_call x1, Pallas kernels, local(): pl.pallas_call(finish, out_shape=(jax.ShapeDtypeStruct((VOCAB_DEV, COLS),...  4.3 us

profile of v4, /device:TPU:1, one launch (start us, length us, event | category | flops | bytes accessed | tf_op | source)
XLA Modules:
  0.0 46.4 jit_solution(2712210083414316455)
XLA Ops:
  0.6 41.3 %exchange.1 = (f32[8064,256]{1,0:T(8,128)S(1)}, bf16[16,32,256]{2,1,0:T(8,128)(2,1)S(1)}, s32[32,128]{1,0:T(8,128)S(1)}, f32[64,128]{1,0:T(8,128)S(1)}) custom-call(bf16[128,4096]{1,0:T(8,128)(2,1)} %grads_hbm.1, s32[1,128]{1,0:T(1,128)} %bitcast.3), custom_call_target="tpu_custom_call" | custom-call | tf_op jit(solution)/shard_map/exchange/pallas_call | solution.py:200
  41.9 4.3 %finish.1 = (f32[8016,256]{1,0:T(8,128)}, f32[64,128]{1,0:T(8,128)}) custom-call(f32[8064,256]{1,0:T(8,128)S(1)} %get-tuple-element.8.table_ref, bf16[16,32,256]{2,1,0:T(8,128)(2,1)S(1)} %get-tuple-element.9.last_ref, s32[32,128]{1,0:T(8,128)S(1)} %get-tuple-element.10.keys_ref, f32[64,128]{1,0:T(8,128)S(1)} %get-tuple-element.11.share_ref), custom_call_target="tpu_custom_call" | custom-call | tf_op jit(solution)/shard_map/finish/pallas_call | solution.py:226

commit v5 on v4

--- a/solution.py
+++ b/solution.py
@@ -15,7 +15,7 @@
 HI_ROWS = 64
 PAD_ROWS = 8064
 STRIPE = 4032
-PIECES = (1344,) * 5 + (1296,)
+PIECES = (336, 1008) + (1344,) * 4 + (1296,)
 MESH = pl.DeviceIdType.MESH
 NT = (((1,), (1,)), ((), ()))
 

time: 46.5 us -> 46.4 us (level)
  no operation moved by 1% of the time
where the time goes in v5:
time: 46.4 us; the launch traced here: 46.3 us
  Pallas kernels  45.5 us (98%)
  between operations  0.8 us (2%)
    pallas_call x1, Pallas kernels, local(): pl.pallas_call(exchange, out_shape=(pltpu.VMEM((PAD_ROWS, COLS), jnp.floa...  41.3 us
    pallas_call x1, Pallas kernels, local(): pl.pallas_call(finish, out_shape=(jax.ShapeDtypeStruct((VOCAB_DEV, COLS),...  4.22 us

profile of v5, /device:TPU:1, one launch (start us, length us, event | category | flops | bytes accessed | tf_op | source)
XLA Modules:
  0.0 46.3 jit_solution(6057460993719110212)
XLA Ops:
  0.6 41.3 %exchange.1 = (f32[8064,256]{1,0:T(8,128)S(1)}, bf16[16,32,256]{2,1,0:T(8,128)(2,1)S(1)}, s32[32,128]{1,0:T(8,128)S(1)}, f32[64,128]{1,0:T(8,128)S(1)}) custom-call(bf16[128,4096]{1,0:T(8,128)(2,1)} %grads_hbm.1, s32[1,128]{1,0:T(1,128)} %bitcast.3), custom_call_target="tpu_custom_call" | custom-call | tf_op jit(solution)/shard_map/exchange/pallas_call | solution.py:200
  41.9 4.2 %finish.1 = (f32[8016,256]{1,0:T(8,128)}, f32[64,128]{1,0:T(8,128)}) custom-call(f32[8064,256]{1,0:T(8,128)S(1)} %get-tuple-element.8.table_ref, bf16[16,32,256]{2,1,0:T(8,128)(2,1)S(1)} %get-tuple-element.9.last_ref, s32[32,128]{1,0:T(8,128)S(1)} %get-tuple-element.10.keys_ref, f32[64,128]{1,0:T(8,128)S(1)} %get-tuple-element.11.share_ref), custom_call_target="tpu_custom_call" | custom-call | tf_op jit(solution)/shard_map/finish/pallas_call | solution.py:226
